TPU v7x, 32 devices: a whole 2x2x4 slice. The times are simulated.
32 devices in a mesh: grp: 2 (over x), seq: 16 (over z, y, core).
Axes of the slice: x: 2, y: 2, z: 4, core: 2. Of those that a mesh axis runs over, the one named last changes fastest.
Arguments:
- queries: bfloat16 [8, 4096], P('grp', 'seq'), parts along dimension 0, may hold values from -40 to 40
- gate_logits: float32 [8, 64], P('grp'), parts along dimension 0, may hold values from -6 to 6
- kv_pool: bfloat16 [512, 128, 2048], P(('grp', 'seq')), parts along dimension 0, may hold values from -6 to 6
- page_table: int32 [8, 64], P('grp'), parts along dimension 0, may hold values from 0 to 255, as said below
- selected: int32 [8, 8, 16], P('grp'), parts along dimension 0, may hold values from 0 to 63, as said below
- lengths: int32 [8], P('grp'), parts along dimension 0, may hold values from 4096 to 8192, as said below
Outputs:
- attended: bfloat16 [8, 4096], P('grp', 'seq'), parts along dimension 0
There are 2 independent parts, one for each index of `grp`. A program takes and returns all parts, laid end to end along the dimension named above; each array names one. Nothing has to cross between parts.
Inputs may be any that keep to these rules, and one draw needn't show every extreme that they name: `page_table`: a one-to-one map of the 4 x 64 pages onto the pool slots; each aligned run of 2 pages of a request lies in 2 consecutive slots starting at a multiple of 2. `lengths`: some request in every draw has length 8192. `selected`: for each request and key-value head, 16 different pages, all among the request's last 32 live pages, the last live page among them.
All inputs are finite; a program needn't handle non-finite values.
Results may differ from a plain program's by a relative error of at most 0.0039.
Values may be sent and summed in bfloat16 or wider, within the bound.
A program may use at most 64 MiB of HBM per device.

v0:
```python
import math

import jax
import jax.numpy as jnp
from jax import lax
from jax.sharding import PartitionSpec as P

HEAD_DIM = 128


neg_big = -1e30


def joined(part, axis, combine):
    gathered = jax.tree.map(lambda a: lax.all_gather(a, axis), part)

    def take(source):
        return jax.tree.map(lambda a: lax.dynamic_index_in_dim(a, source, 0, False), gathered)

    return lax.fori_loop(
        1, lax.axis_size(axis), lambda source, state: combine(state, take(source)), take(0)
    )


def merge_pair(left, right):
    merged = ()
    for offset in (0, 3):
        row_top = jnp.maximum(left[offset], right[offset])
        left_scale = jnp.exp(left[offset] - row_top)
        right_scale = jnp.exp(right[offset] - row_top)
        merged = merged + (
            row_top,
            left[offset + 1] * left_scale + right[offset + 1] * right_scale,
            left[offset + 2] * left_scale[..., None] + right[offset + 2] * right_scale[..., None],
        )
    return merged


def per_device(queries, gate_logits, kv_pool, page_table, selected, lengths):
    slot_count, page_len, double_width = kv_pool.shape
    kv_width = double_width // 2
    kv_heads = kv_width // HEAD_DIM
    requests = page_table.shape[0]
    ctx_pages = page_table.shape[1]
    col_count = queries.shape[1]
    highest = lax.Precision.HIGHEST
    all_queries = lax.all_gather(queries, "seq", axis=1, tiled=True)
    head_count = all_queries.shape[1] // HEAD_DIM
    group_size = head_count // kv_heads
    score_scale = 1.0 / math.sqrt(HEAD_DIM)
    first_slot = lax.axis_index("seq") * slot_count
    slot_ids = first_slot + jnp.arange(slot_count, dtype=jnp.int32)
    slot_match = page_table[:, :, None] == slot_ids[None, None, :]
    owner_hot = jnp.any(slot_match, axis=1)
    page_index = jnp.arange(ctx_pages, dtype=jnp.int32)
    page_of = jnp.sum(jnp.where(slot_match, page_index[None, :, None], 0), axis=(0, 1))
    slot_len = jnp.sum(jnp.where(owner_hot, lengths[:, None], 0), axis=0)
    owner_rows = jnp.dot(
        owner_hot.T.astype(jnp.bfloat16), all_queries, preferred_element_type=jnp.float32
    ).astype(jnp.bfloat16)
    slot_queries = owner_rows.reshape(slot_count, kv_heads, group_size, HEAD_DIM)
    key_rows = kv_pool[:, :, :kv_width].reshape(slot_count, page_len, kv_heads, HEAD_DIM)
    value_rows = kv_pool[:, :, kv_width:].reshape(slot_count, page_len, kv_heads, HEAD_DIM)
    position = page_of[:, None] * page_len + jnp.arange(page_len, dtype=jnp.int32)[None, :]
    is_valid = position < slot_len[:, None]
    is_live = page_of * page_len < slot_len
    valid_bf = is_valid.astype(jnp.bfloat16)
    counts = jnp.maximum(jnp.sum(is_valid.astype(jnp.float32), axis=1), 1.0)
    summary_keys = (
        jnp.einsum("st,stkd->skd", valid_bf, key_rows, preferred_element_type=jnp.float32)
        / counts[:, None, None]
    ).astype(jnp.bfloat16)
    summary_values = (
        jnp.einsum("st,stkd->skd", valid_bf, value_rows, preferred_element_type=jnp.float32)
        / counts[:, None, None]
    ).astype(jnp.bfloat16)
    coarse = (
        jnp.einsum("skgd,skd->skg", slot_queries, summary_keys, preferred_element_type=jnp.float32)
        * score_scale
    )
    coarse_mask = owner_hot[:, :, None, None] & is_live[None, :, None, None]
    coarse_masked = jnp.where(coarse_mask, coarse[None], neg_big)
    coarse_top = jnp.max(coarse_masked, axis=1)
    coarse_wt = jnp.where(coarse_mask, jnp.exp(coarse_masked - coarse_top[:, None]), 0.0)
    coarse_sum = jnp.sum(coarse_wt, axis=1)
    coarse_num = jnp.einsum(
        "rskg,skd->rkgd", coarse_wt, summary_values.astype(jnp.float32), precision=highest
    )
    fine_scores = (
        jnp.einsum("skgd,stkd->skgt", slot_queries, key_rows, preferred_element_type=jnp.float32)
        * score_scale
    )
    token_mask = is_valid[:, None, None, :]
    fine_masked = jnp.where(token_mask, fine_scores, neg_big)
    page_max = jnp.max(fine_masked, axis=3)
    page_wt = jnp.where(token_mask, jnp.exp(fine_masked - page_max[..., None]), 0.0).astype(
        jnp.bfloat16
    )
    page_sum = jnp.sum(page_wt.astype(jnp.float32), axis=3)
    page_num = jnp.einsum(
        "skgt,stkd->skgd", page_wt, value_rows, preferred_element_type=jnp.float32
    )
    page_hit = selected[:, None, :, :] == page_of[None, :, None, None]
    chosen = jnp.any(page_hit, axis=3) & owner_hot[:, :, None]
    chosen_full = chosen[..., None]
    sel_masked = jnp.where(chosen_full, page_max[None], neg_big)
    fine_top = jnp.max(sel_masked, axis=1)
    fine_wt = jnp.where(chosen_full, jnp.exp(sel_masked - fine_top[:, None]), 0.0)
    fine_sum = jnp.sum(fine_wt * page_sum[None], axis=1)
    fine_num = jnp.einsum("rskg,skgd->rkgd", fine_wt, page_num, precision=highest)
    gate_all = jax.nn.sigmoid(gate_logits)
    start_col = lax.axis_index("seq") * col_count
    coarse_gate = lax.dynamic_slice_in_dim(
        jnp.repeat(gate_all[:, :head_count], HEAD_DIM, axis=1), start_col, col_count, 1
    )
    fine_gate = lax.dynamic_slice_in_dim(
        jnp.repeat(gate_all[:, head_count:], HEAD_DIM, axis=1), start_col, col_count, 1
    )
    merged = joined(
        (coarse_top, coarse_sum, coarse_num, fine_top, fine_sum, fine_num), "seq", merge_pair
    )
    coarse_full = (merged[2] / merged[1][..., None]).reshape(requests, head_count * HEAD_DIM)
    fine_full = (merged[5] / merged[4][..., None]).reshape(requests, head_count * HEAD_DIM)
    coarse_cols = lax.dynamic_slice_in_dim(coarse_full, start_col, col_count, 1)
    fine_cols = lax.dynamic_slice_in_dim(fine_full, start_col, col_count, 1)
    return (coarse_gate * coarse_cols + fine_gate * fine_cols).astype(jnp.bfloat16)


def solution(mesh):
    return jax.shard_map(
        per_device,
        mesh=mesh,
        in_specs=(
            P("grp", "seq"),
            P("grp", None),
            P(("grp", "seq"), None, None),
            P("grp", None),
            P("grp", None, None),
            P("grp"),
        ),
        out_specs=P("grp", "seq"),
        check_vma=False,
    )
```

profile of v0, /device:TPU:0, one launch (start us, length us, event | category | flops | bytes accessed | tf_op | source)
XLA Modules:
  0.0 191.3 jit_solution(17139264196177832659)
XLA Ops:
  6.5 0.9 compare_reduce_fusion.1
  7.4 0.9 fusion.21
  9.3 23.4 %all_gather.39 = bf16[4,4096]{1,0:T(4,128)(2,1)S(1)} all-gather(bf16[4,256]{1,0:T(4,128)(2,1)} %param.8), channel_id=1, replica_groups=mesh['grp'=2,'seq'=16] {'seq'}, dimensions={1}, use_global_device_ids=true | all-gather | bytes 34816 | tf_op jit(solution)/shard_map/all_gather | solution.py:47
  33.1 6.1 %fusion.43 = (bf16[16,128,1024]{2,1,0:T(8,128)(2,1)}, bf16[16,128,1024]{2,1,0:T(8,128)(2,1)}) fusion(bf16[16,128,2048]{2,1,0:T(8,128)(2,1)} %param.10), kind=kLoop, calls=%fused_computation.82 | loop fusion | bytes 16777216 | tf_op jit(solution)/shard_map/slice | solution.py:63
  39.2 6.4 %copy.115 = bf16[16,128,1024]{1,2,0:T(8,128)(2,1)} copy(bf16[16,128,1024]{2,1,0:T(8,128)(2,1)} %get-tuple-element.421) | data formatting | bytes 8388608
  45.6 6.4 %copy.114 = bf16[16,128,1024]{1,2,0:T(8,128)(2,1)} copy(bf16[16,128,1024]{2,1,0:T(8,128)(2,1)} %get-tuple-element.422) | data formatting | bytes 8388608
  52.0 3.5 %fusion.31 = f32[16,1,8,128]{3,1,2,0:T(1,128)S(1)} fusion(bf16[16,128,8,128]{1,3,2,0:T(8,128)(2,1)} %bitcast.92, pred[16,128,1,1]{1,0,2,3:T(8,128)(4,1)S(1)} %get-tuple-element.428), kind=kOutput, calls=%fused_computation.61 | convolution fusion | flops 4194304 | bytes 4261888 | tf_op jit(solution)/shard_map/st,stkd->skd/dot_general | solution.py:74
  55.5 1.2 fusion.33
  57.6 0.9 fusion.22
  58.5 1.2 compare_reduce_fusion
  59.9 3.5 %fusion.45 = (f32[16,8,4]{2,1,0:T(8,128)S(1)}, f32[16,8,4,128]{3,2,1,0:T(4,128)S(1)}) fusion(bf16[16,8,4,128]{3,2,1,0:T(4,128)(2,1)S(1)} %reshape.105, bf16[16,128,8,128]{1,3,2,0:T(8,128)(2,1)} %bitcast.94, pred[16,128]{1,0:T(8,128)(4,1)S(1)} %get-tuple-element.427), kind=kOutput, calls=%fused_computation.84 | convolution fusion | flops 16973312 | bytes 4591616 | tf_op jit(solution)/shard_map/skgd,stkd->skgt/dot_general | solution.py:90
  63.7 4.5 %fusion.40 = f32[16,8,4,128]{3,2,1,0:T(4,128)S(1)} fusion(bf16[16,128,8,128]{1,3,2,0:T(8,128)(2,1)} %bitcast.93, f32[16,8,4,128]{3,2,1,0:T(4,128)S(1)} %get-tuple-element.430, f32[16,8,4]{2,1,0:T(8,128)S(1)} %get-tuple-element.429, pred[16,128]{1,0:T(8,128)(4,1)S(1)} %get-tuple-element.427), kind=kOutput, calls=%fused_computation.81 | convolution fusion | flops 16973824 | bytes 4722688 | tf_op jit(solution)/shard_map/skgt,stkd->skgd/dot_general | solution.py:100
  70.9 18.0 %all-gather.1 = f32[64,8,4]{1,2,0:T(4,128)S(1)} all-gather(f32[4,8,4]{1,2,0:T(4,128)S(1)} %copy.87), channel_id=3, replica_groups=mesh['grp'=2,'seq'=16] {'seq'}, dimensions={0}, use_global_device_ids=true | all-gather | bytes 8704 | tf_op jit(solution)/shard_map/all_gather | solution.py:15
  88.9 19.0 %all-gather = f32[64,8,4]{1,2,0:T(4,128)S(1)} all-gather(f32[4,8,4]{1,2,0:T(4,128)S(1)} %copy.86), channel_id=2, replica_groups=mesh['grp'=2,'seq'=16] {'seq'}, dimensions={0}, use_global_device_ids=true | all-gather | bytes 8704 | tf_op jit(solution)/shard_map/all_gather | solution.py:15
  107.9 18.0 %all-gather.4 = f32[64,8,4]{1,2,0:T(4,128)S(1)} all-gather(f32[4,8,4]{1,2,0:T(4,128)S(1)} %copy.95), channel_id=6, replica_groups=mesh['grp'=2,'seq'=16] {'seq'}, dimensions={0}, use_global_device_ids=true | all-gather | bytes 8704 | tf_op jit(solution)/shard_map/all_gather | solution.py:15
  125.9 19.0 %all-gather.3 = f32[64,8,4]{1,2,0:T(4,128)S(1)} all-gather(f32[4,8,4]{1,2,0:T(4,128)S(1)} %copy.93), channel_id=5, replica_groups=mesh['grp'=2,'seq'=16] {'seq'}, dimensions={0}, use_global_device_ids=true | all-gather | bytes 8704 | tf_op jit(solution)/shard_map/all_gather | solution.py:15
  146.7 36.7 %while.25 = (s32[]{:T(128)}, f32[4,8,4]{1,2,0:T(4,128)S(1)}, f32[4,8,4]{1,2,0:T(4,128)S(1)}, f32[4,8,4,128]{3,2,1,0:T(4,128)S(1)}, f32[4,8,4]{1,2,0:T(4,128)S(1)...) while((s32[]{:T(128)}, f32[4,8,4]{1,2,0:T(4,128)S(1)}, ...), condition=%wide.region_12.13_spmd, body=%wide.region_11.12_spmd.sunk | while | flops 99845 | bytes 538823 | solution.py:20
  148.0 1.1 fusion.60
  150.4 1.1 fusion.60
  152.9 1.1 fusion.60
  155.3 1.1 fusion.60
  157.8 1.1 fusion.60
  160.2 1.1 fusion.60
  162.7 1.1 fusion.60
  165.1 1.1 fusion.60
  167.6 1.1 fusion.60
  170.0 1.1 fusion.60
  172.5 1.1 fusion.60
  174.9 1.1 fusion.60
  177.4 1.1 fusion.60
  179.8 1.1 fusion.60
  182.3 1.1 fusion.60
  (166 shorter events, 27.5 us)
Async XLA Ops:
  6.5 138.4 %all-gather.9.cloned.1.call-start = ((), (), s32[]{:S(2)}) async-start(), calls=%async_computation | async-start | bytes 1114112 | tf_op jit(solution)/shard_map/all_gather | solution.py:15
  52.0 3.5 %copy-start = (bf16[16,128,1024]{1,2,0:T(8,128)(2,1)S(1)}, bf16[16,128,1024]{1,2,0:T(8,128)(2,1)}, u32[]{:S(2)}) copy-start(bf16[16,128,1024]{1,2,0:T(8,128)(2,1)} %copy.114) | copy-start | bytes 12582916
  52.0 6.5 %copy-start.1 = (s32[4,8,16]{2,1,0:T(8,128)S(1)}, s32[4,8,16]{2,1,0:T(8,128)}, u32[]{:S(2)}) copy-start(s32[4,8,16]{2,1,0:T(8,128)} %param.12) | copy-start | bytes 6148
  58.5 87.3 %all-gather.11.cloned.1.call-start = ((), (), s32[]{:S(2)}) async-start(), calls=%async_computation.1 | async-start | bytes 1114112 | tf_op jit(solution)/shard_map/all_gather | solution.py:15
  59.9 9.7 %copy-start.2 = (f32[4,64]{1,0:T(4,128)S(1)}, f32[4,64]{1,0:T(4,128)}, u32[]{:S(2)}) copy-start(f32[4,64]{1,0:T(4,128)} %param.9) | copy-start | bytes 3076
Sparse Core Ops, SparseCore 0:
  58.6 34.1 all-gather.8
  94.9 37.5 all-gather.10
where the time goes:
time: 193 us; the launch traced here: 191 us
  blocking collectives  97.5 us (51%)
  local copies, waits for them, and re-layouts  41.4 us (21%)
  other arithmetic  23.8 us (12%)
  matrix products  14.6 us (8%)
  between operations  13.6 us (7%)
    all_gather x4, blocking collectives, joined(): gathered = jax.tree.map(lambda a: lax.all_gather(a, axis), part)  74 us
    all_gather x1, blocking collectives, per_device(): all_queries = lax.all_gather(queries, 'seq', axis=1, tiled=True)  23.4 us
    add x15, other arithmetic, merge_pair(): left[offset + 2] * left_scale[..., None]  16.9 us
    dynamic_slice x21, local copies, waits for them, and re-layouts, take(): lax.dynamic_index_in_dim(a, source, 0, False)  14.4 us
    unnamed x11, local copies, waits for them, and re-layouts  13 us
    slice x1, local copies, waits for them, and re-layouts, per_device(): kv_pool[:, :, kv_width:].reshape(slot_count, page_len, kv_heads, HEAD_DIM)  6.11 us
    dot_general x1, matrix products, per_device(): jnp.einsum('skgt,stkd->skgd', page_wt, value_rows, preferred_element_type...  4.5 us
  transfers between devices with their start and end apart: 2, of which 0 were waited for; matrix products, arithmetic and copies ran while one was open for 7% of the time, Pallas kernels for 0%

commit v1 on v0

--- a/solution.py
+++ b/solution.py
@@ -1,8 +1,11 @@
+import functools
 import math
 
 import jax
 import jax.numpy as jnp
 from jax import lax
+from jax.experimental import pallas as pl
+from jax.experimental.pallas import tpu as pltpu
 from jax.sharding import PartitionSpec as P
 
 HEAD_DIM = 128
@@ -36,7 +39,7 @@
     return merged
 
 
-def per_device(queries, gate_logits, kv_pool, page_table, selected, lengths):
+def per_device_plain(queries, gate_logits, kv_pool, page_table, selected, lengths):
     slot_count, page_len, double_width = kv_pool.shape
     kv_width = double_width // 2
     kv_heads = kv_width // HEAD_DIM
@@ -126,6 +129,285 @@
     return (coarse_gate * coarse_cols + fine_gate * fine_cols).astype(jnp.bfloat16)
 
 
+RUN = 2
+MESH = pl.DeviceIdType.MESH
+F32 = jnp.float32
+BF16 = jnp.bfloat16
+
+
+def fused_kernel(
+    n, q_hbm, gate_hbm, kv_hbm, pt_hbm, sel_hbm, len_hbm, out_ref,
+    kv_buf, q_all, gate_v, pt_v, sel_v, len_s, q_even, gather_f, send_buf, recv_buf,
+    kv_sem, in_sem, q_send, q_recv, p_send, p_recv,
+):
+    me = lax.axis_index("seq")
+    slots, page_len, width = kv_buf.shape
+    kv_width = width // 2
+    kv_heads = kv_width // HEAD_DIM
+    runs = slots // RUN
+    span = RUN * page_len
+    requests, ctx = pt_v.shape
+    per_dev = q_all.shape[2] // HEAD_DIM
+    heads = per_dev * n
+    group = heads // kv_heads
+    scale = math.log2(math.e) / math.sqrt(HEAD_DIM)
+
+    def load_run(j):
+        return pltpu.make_async_copy(
+            kv_hbm.at[pl.ds(j * RUN, RUN)], kv_buf.at[pl.ds(j * RUN, RUN)], kv_sem.at[j]
+        )
+
+    small = [
+        pltpu.make_async_copy(q_hbm, q_all.at[me], in_sem.at[0]),
+        pltpu.make_async_copy(pt_hbm, pt_v, in_sem.at[1]),
+        pltpu.make_async_copy(len_hbm, len_s, in_sem.at[2]),
+        pltpu.make_async_copy(sel_hbm, sel_v, in_sem.at[3]),
+        pltpu.make_async_copy(gate_hbm, gate_v, in_sem.at[4]),
+    ]
+    barrier = pltpu.get_barrier_semaphore()
+    peers = [lax.rem(me + step, n) for step in range(1, n)]
+    for peer in peers:
+        pl.semaphore_signal(barrier, inc=1, device_id={"seq": peer}, device_id_type=MESH)
+    for copy in small:
+        copy.start()
+    for j in range(runs):
+        load_run(j).start()
+    small[0].wait()
+    pl.semaphore_wait(barrier, n - 1)
+
+    def q_copy(slot, peer):
+        return pltpu.make_async_remote_copy(
+            src_ref=q_all.at[slot], dst_ref=q_all.at[slot], send_sem=q_send.at[peer],
+            recv_sem=q_recv.at[slot], device_id={"seq": peer}, device_id_type=MESH,
+        )
+
+    for peer in peers:
+        q_copy(me, peer).start()
+    for copy in small[1:]:
+        copy.wait()
+
+    table = pt_v[...]
+    row_id = lax.broadcasted_iota(jnp.int32, (requests, ctx), 0)
+    col_f = lax.broadcasted_iota(jnp.int32, (requests, ctx), 1).astype(F32)
+    len_grid = jnp.zeros((requests, ctx), F32)
+    for r in range(requests):
+        len_grid = jnp.where(row_id == r, len_s[r].astype(F32), len_grid)
+    head_row = lax.broadcasted_iota(jnp.int32, (heads, 1), 0)
+    head_id = lax.rem(head_row, n) * per_dev + head_row // n
+    kv_row = head_id // group
+    chosen_ids = []
+    for r in range(requests):
+        ids = sel_v[r].astype(F32)
+        wide = jnp.zeros((heads, ids.shape[1]), F32)
+        for k in range(kv_heads):
+            wide = jnp.where(kv_row == k, ids[k : k + 1, :], wide)
+        chosen_ids.append(wide)
+    lane = lax.broadcasted_iota(jnp.int32, (1, span), 1)
+    lane_f = lane.astype(F32)
+    hot, valid, fine_ok, live, count = [], [], [], [], []
+    for j in range(runs):
+        match = table == me * slots + j * RUN
+        page = jnp.sum(jnp.where(match, col_f, 0.0), axis=(0, 1), keepdims=True)
+        length = jnp.sum(jnp.where(match, len_grid, 0.0), axis=(0, 1), keepdims=True)
+        owner = jnp.max(jnp.where(match, 1.0, 0.0), axis=1, keepdims=True)
+        hot_j = [owner[r : r + 1, :] for r in range(requests)]
+        ids = chosen_ids[0] * hot_j[0]
+        for r in range(1, requests):
+            ids = ids + chosen_ids[r] * hot_j[r]
+        valid_j = jnp.where(page * page_len + lane_f < length, 1.0, 0.0)
+        ok = jnp.zeros((heads, span), F32)
+        live_j, count_j = [], []
+        for e in range(RUN):
+            hit = jnp.max(jnp.where(ids == page + e, 1.0, 0.0), axis=1, keepdims=True)
+            ok = jnp.where(lane // page_len == e, hit, ok)
+            left = length - (page + e) * page_len
+            live_j.append(jnp.where(left > 0.0, 1.0, 0.0))
+            count_j.append(jnp.clip(left, 1.0, float(page_len)))
+        hot.append(hot_j)
+        valid.append(valid_j)
+        fine_ok.append(ok * valid_j)
+        live.append(live_j)
+        count.append(count_j)
+
+    for step, peer in enumerate(peers):
+        q_copy(peer, peer).wait_recv()
+    for src in range(n):
+        rows = q_all[src].astype(F32)
+        for w in range(per_dev):
+            q_even[w, src * requests : (src + 1) * requests, :] = rows[
+                :, w * HEAD_DIM : (w + 1) * HEAD_DIM
+            ]
+    q_rows = [
+        jnp.concatenate(
+            [q_even[w, pl.ds(r, n, stride=requests), :] for w in range(per_dev)], axis=0
+        )
+        for r in range(requests)
+    ]
+
+    fine_m, fine_l, fine_n, coarse_s, coarse_v = [], [], [], [], []
+    valid_rows = 16
+    row16 = lax.broadcasted_iota(jnp.int32, (valid_rows, span), 0)
+    for j in range(runs):
+        q_j = q_rows[0] * hot[j][0]
+        for r in range(1, requests):
+            q_j = q_j + q_rows[r] * hot[j][r]
+        q_bd = jnp.concatenate(
+            [jnp.where(kv_row == k, q_j, 0.0) for k in range(kv_heads)], axis=1
+        ).astype(BF16)
+        load_run(j).wait()
+        keys = kv_buf[j * RUN : (j + 1) * RUN, :, :kv_width].reshape(span, kv_width)
+        vals = kv_buf[j * RUN : (j + 1) * RUN, :, kv_width:].reshape(span, kv_width)
+        scores = lax.dot_general(
+            q_bd, keys, (((1,), (1,)), ((), ())), preferred_element_type=F32
+        ) * scale
+        ok = fine_ok[j] > 0.0
+        masked = jnp.where(ok, scores, neg_big)
+        top = jnp.max(masked, axis=1, keepdims=True)
+        wt = jnp.where(ok, jnp.exp2(masked - top), 0.0).astype(BF16)
+        fine_m.append(top)
+        fine_l.append(jnp.sum(wt.astype(F32), axis=1, keepdims=True))
+        shown = scores * valid[j]
+        page_rows = jnp.where(lane // page_len == row16, valid[j], 0.0).astype(BF16)
+        mixed = lax.dot_general(
+            jnp.concatenate([wt, page_rows], axis=0), vals, (((1,), (0,)), ((), ())),
+            preferred_element_type=F32,
+        )
+        num = mixed[:heads, :HEAD_DIM]
+        for k in range(1, kv_heads):
+            num = jnp.where(kv_row == k, mixed[:heads, k * HEAD_DIM : (k + 1) * HEAD_DIM], num)
+        fine_n.append(num)
+        for e in range(RUN):
+            mean = jnp.sum(
+                shown[:, e * page_len : (e + 1) * page_len], axis=1, keepdims=True
+            ) / count[j][e]
+            coarse_s.append(jnp.where(live[j][e] > 0.0, mean, neg_big))
+            sv = (mixed[heads + e : heads + e + 1, :] / count[j][e]).astype(BF16).astype(F32)
+            wide = jnp.broadcast_to(sv[:, :HEAD_DIM], (heads, HEAD_DIM))
+            for k in range(1, kv_heads):
+                wide = jnp.where(kv_row == k, sv[:, k * HEAD_DIM : (k + 1) * HEAD_DIM], wide)
+            coarse_v.append(wide)
+
+    unit = 2 * per_dev * requests
+    lane_row = lax.broadcasted_iota(jnp.int32, (heads, HEAD_DIM), 1)
+
+    def put(kind, r, top, total, num):
+        top_b = top.astype(BF16).astype(F32)
+        high = total.astype(BF16).astype(F32)
+        stat = jnp.where(lane_row == 0, top_b, jnp.where(lane_row == 1, high, total - high))
+        for w in range(per_dev):
+            row = kind * per_dev * requests + w * requests + r
+            gather_f[pl.ds(row, n, stride=2 * unit), :] = num[w * n : (w + 1) * n]
+            gather_f[pl.ds(unit + row, n, stride=2 * unit), :] = stat[w * n : (w + 1) * n]
+
+    for r in range(requests):
+        for kind in range(2):
+            if kind == 0:
+                tops = coarse_s
+                owner = [hot[i // RUN][r] for i in range(slots)]
+            else:
+                tops = fine_m
+                owner = [hot[j][r] for j in range(runs)]
+            held = [jnp.where(o > 0.0, t, neg_big) for o, t in zip(owner, tops)]
+            top = functools.reduce(jnp.maximum, held)
+            top = top.astype(BF16).astype(F32)
+            total = jnp.zeros((heads, 1), F32)
+            num = jnp.zeros((heads, HEAD_DIM), F32)
+            for i, h in enumerate(held):
+                weight = jnp.where(h > 0.5 * neg_big, jnp.exp2(h - top), 0.0)
+                if kind == 0:
+                    total = total + weight
+                    num = num + weight * coarse_v[i]
+                else:
+                    total = total + weight * fine_l[i]
+                    num = num + weight * fine_n[i]
+            put(kind, r, top, total, num)
+    for d in range(n):
+        send_buf[d] = gather_f[d * 2 * unit : (d + 1) * 2 * unit, :].astype(BF16)
+
+    def p_copy(slot, peer):
+        return pltpu.make_async_remote_copy(
+            src_ref=send_buf.at[peer], dst_ref=recv_buf.at[slot], send_sem=p_send.at[peer],
+            recv_sem=p_recv.at[slot], device_id={"seq": peer}, device_id_type=MESH,
+        )
+
+    for peer in peers:
+        p_copy(me, peer).start()
+    recv_buf[me] = send_buf[me]
+    gates = jax.nn.sigmoid(gate_v[...])
+    gate_lane = lax.broadcasted_iota(jnp.int32, gates.shape, 1)
+    gate_col = [
+        [
+            jnp.sum(
+                jnp.where(gate_lane == kind * heads + me * per_dev + w, gates, 0.0),
+                axis=1, keepdims=True,
+            )
+            for w in range(per_dev)
+        ]
+        for kind in range(2)
+    ]
+    for peer in peers:
+        p_copy(peer, peer).wait_recv()
+    stats = [recv_buf[src, unit:, :].astype(F32) for src in range(n)]
+    tops = [s[:, 0:1] for s in stats]
+    top = functools.reduce(jnp.maximum, tops)
+    total = jnp.zeros((unit, 1), F32)
+    num = jnp.zeros((unit, HEAD_DIM), F32)
+    for src in range(n):
+        weight = jnp.exp2(tops[src] - top)
+        total = total + weight * (stats[src][:, 1:2] + stats[src][:, 2:3])
+        num = num + weight * recv_buf[src, :unit, :].astype(F32)
+    full = num / total
+    for w in range(per_dev):
+        c_row = w * requests
+        f_row = per_dev * requests + w * requests
+        out_ref[:, w * HEAD_DIM : (w + 1) * HEAD_DIM] = (
+            gate_col[0][w] * full[c_row : c_row + requests]
+            + gate_col[1][w] * full[f_row : f_row + requests]
+        ).astype(BF16)
+    for peer in peers:
+        q_copy(me, peer).wait_send()
+        p_copy(me, peer).wait_send()
+
+
+def per_device(queries, gate_logits, kv_pool, page_table, selected, lengths):
+    n = lax.axis_size("seq")
+    slots, page_len, width = kv_pool.shape
+    requests, cols = queries.shape
+    if cols % HEAD_DIM != 0:
+        return per_device_plain(queries, gate_logits, kv_pool, page_table, selected, lengths)
+    per_dev = cols // HEAD_DIM
+    unit = 2 * per_dev * requests
+    dma = pltpu.SemaphoreType.DMA
+    return pl.pallas_call(
+        functools.partial(fused_kernel, n),
+        out_shape=jax.ShapeDtypeStruct((requests, cols), BF16),
+        in_specs=[pl.BlockSpec(memory_space=pltpu.HBM)] * 6,
+        out_specs=pl.BlockSpec(memory_space=pltpu.VMEM),
+        scratch_shapes=[
+            pltpu.VMEM(kv_pool.shape, BF16),
+            pltpu.VMEM((n, requests, cols), BF16),
+            pltpu.VMEM(gate_logits.shape, F32),
+            pltpu.VMEM(page_table.shape, jnp.int32),
+            pltpu.VMEM(selected.shape, jnp.int32),
+            pltpu.SMEM(lengths.shape, jnp.int32),
+            pltpu.VMEM((per_dev, n * requests, HEAD_DIM), F32),
+            pltpu.VMEM((n * 2 * unit, HEAD_DIM), F32),
+            pltpu.VMEM((n, 2 * unit, HEAD_DIM), BF16),
+            pltpu.VMEM((n, 2 * unit, HEAD_DIM), BF16),
+            dma((slots // RUN,)),
+            dma((5,)),
+            dma((n,)),
+            dma((n,)),
+            dma((n,)),
+            dma((n,)),
+        ],
+        compiler_params=pltpu.CompilerParams(
+            collective_id=0, has_side_effects=True, vmem_limit_bytes=48 * 1024 * 1024
+        ),
+        name="paged_sparse_decode",
+    )(queries, gate_logits, kv_pool, page_table, selected, lengths)
+
+
 def solution(mesh):
     return jax.shard_map(
         per_device,

time: 193 us -> 25.9 us (0.13)
  blocking collectives: 97.5 us -> 0 us
  local copies, waits for them, and re-layouts: 41.4 us -> 4 us
  other arithmetic: 23.8 us -> 0 us
  Pallas kernels: 0 us -> 21.5 us
  matrix products: 14.6 us -> 0 us
  between operations: 13.6 us -> 0.01 us
    all_gather x5 -> x0, blocking collectives: 97.5 us -> none  [the longest x4 74 us: joined(): gathered = jax.tree.map(lambda a: lax.all_gather(a, axis), part)]
    pallas_call x0 -> x1, Pallas kernels: none -> 21.5 us  [per_device(): pl.pallas_call(functools.partial(fused_kernel, n), out_shape=jax.ShapeDty...]
    add x46 -> x0, other arithmetic: 17.7 us -> none  [the longest x15 16.9 us: merge_pair(): left[offset + 2] * left_scale[..., None]]
    dynamic_slice x21 -> x0, local copies, waits for them, and re-layouts: 14.4 us -> none  [take(): lax.dynamic_index_in_dim(a, source, 0, False)]
    dot_general x7 -> x0, matrix products: 13.8 us -> none  [the longest x1 4.5 us: per_device(): jnp.einsum('skgt,stkd->skgd', page_wt, value_rows, preferred_element_type...]
    unnamed x11, local copies, waits for them, and re-layouts: 13 us -> 4 us
    slice x2 -> x0, local copies, waits for them, and re-layouts: 6.19 us -> none  [the longest x1 6.11 us: per_device(): kv_pool[:, :, kv_width:].reshape(slot_count, page_len, kv_heads, HEAD_DIM)]
    exp x60 -> x0, local copies, waits for them, and re-layouts: 5.89 us -> none  [the longest x30 2.95 us: merge_pair(): right_scale = jnp.exp(right[offset] - row_top)]
  transfers between devices with their start and end apart: 2 -> 0, of which waited for: 0 -> 0; matrix products, arithmetic and copies ran while one was open for 7% -> 0% of each run, Pallas kernels for 0% -> 0%
where the time goes in v1:
time: 25.9 us; the launch traced here: 25.5 us
  Pallas kernels  21.5 us (83%)
  local copies, waits for them, and re-layouts  4 us (15%)
    pallas_call x1, Pallas kernels, per_device(): pl.pallas_call(functools.partial(fused_kernel, n), out_shape=jax.ShapeDty...  21.5 us
    unnamed x11, local copies, waits for them, and re-layouts  4 us

profile of v1, /device:TPU:0, one launch (start us, length us, event | category | flops | bytes accessed | tf_op | source)
XLA Modules:
  0.0 25.5 jit_solution(4892061723172675771)
XLA Ops:
  0.0 0.0 copy-start
  0.0 0.7 %copy-done = s32[4,8,16]{2,1,0:T(8,128)S(1)} copy-done((s32[4,8,16]{2,1,0:T(8,128)S(1)}, s32[4,8,16]{2,1,0:T(8,128)}, u32[]{:S(2)}) %copy-start) | copy-done | bytes 2072
  0.7 0.0 copy-start.1
  0.7 0.7 %copy-done.1 = bf16[4,256]{1,0:T(4,128)(2,1)S(1)} copy-done((bf16[4,256]{1,0:T(4,128)(2,1)S(1)}, bf16[4,256]{1,0:T(4,128)(2,1)}, u32[]{:S(2)}) %copy-start.1) | copy-done | bytes 2072
  1.4 0.0 copy-start.2
  1.4 0.7 %copy-done.2 = f32[4,64]{1,0:T(4,128)S(1)} copy-done((f32[4,64]{1,0:T(4,128)S(1)}, f32[4,64]{1,0:T(4,128)}, u32[]{:S(2)}) %copy-start.2) | copy-done | bytes 1048
  2.1 0.0 copy-start.3
  2.1 0.7 %copy-done.3 = s32[4,64]{1,0:T(4,128)S(1)} copy-done((s32[4,64]{1,0:T(4,128)S(1)}, s32[4,64]{1,0:T(4,128)}, u32[]{:S(2)}) %copy-start.3) | copy-done | bytes 1048
  2.8 0.0 copy-start.4
  2.8 0.7 %copy-done.4 = s32[4]{0:T(128)S(1)} copy-done((s32[4]{0:T(128)S(1)}, s32[4]{0:T(128)}, u32[]{:S(2)}) %copy-start.4) | copy-done | bytes 40
  3.4 21.5 %paged_sparse_decode.1 = bf16[4,256]{1,0:T(4,128)(2,1)S(1)} custom-call(bf16[4,256]{1,0:T(4,128)(2,1)S(1)} %copy-done.1, f32[4,64]{1,0:T(4,128)S(1)} %copy-done.2, bf16[16,128,2048]{2,1,0:T(8,128)(2,1)} %kv_hbm.1, s32[4,64]{1,0:T(4,128)S(1)} %copy-done.3, s32[4,8,16]{2,1,0:T(8,128)S(1)} %copy-done, s32[4]{0:T(128)S(1)} %copy-done.4), custom_call_target="tpu_custom_call" | custom-call | tf_op jit(solution)/shard_map/paged_sparse_decode/pallas_call | solution.py:381
  25.0 0.6 %copy.8 = bf16[4,256]{1,0:T(4,128)(2,1)} copy(bf16[4,256]{1,0:T(4,128)(2,1)S(1)} %paged_sparse_decode.1) | data formatting | bytes 4096
Async XLA Ops:
  0.0 0.7 %copy-start = (s32[4,8,16]{2,1,0:T(8,128)S(1)}, s32[4,8,16]{2,1,0:T(8,128)}, u32[]{:S(2)}) copy-start(s32[4,8,16]{2,1,0:T(8,128)} %sel_hbm.1) | copy-start | bytes 6148
  0.7 0.7 %copy-start.1 = (bf16[4,256]{1,0:T(4,128)(2,1)S(1)}, bf16[4,256]{1,0:T(4,128)(2,1)}, u32[]{:S(2)}) copy-start(bf16[4,256]{1,0:T(4,128)(2,1)} %q_hbm.1) | copy-start | bytes 6148
  1.4 0.7 %copy-start.2 = (f32[4,64]{1,0:T(4,128)S(1)}, f32[4,64]{1,0:T(4,128)}, u32[]{:S(2)}) copy-start(f32[4,64]{1,0:T(4,128)} %gate_hbm.1) | copy-start | bytes 3076
  2.1 0.7 %copy-start.3 = (s32[4,64]{1,0:T(4,128)S(1)}, s32[4,64]{1,0:T(4,128)}, u32[]{:S(2)}) copy-start(s32[4,64]{1,0:T(4,128)} %pt_hbm.1) | copy-start | bytes 3076
  2.8 0.7 %copy-start.4 = (s32[4]{0:T(128)S(1)}, s32[4]{0:T(128)}, u32[]{:S(2)}) copy-start(s32[4]{0:T(128)} %len_hbm.1) | copy-start | bytes 52

commit v2 on v1

--- a/solution.py
+++ b/solution.py
@@ -402,7 +402,7 @@
             dma((n,)),
         ],
         compiler_params=pltpu.CompilerParams(
-            collective_id=0, has_side_effects=True, vmem_limit_bytes=48 * 1024 * 1024
+            collective_id=0, has_side_effects=True, vmem_limit_bytes=67043328
         ),
         name="paged_sparse_decode",
     )(queries, gate_logits, kv_pool, page_table, selected, lengths)

time: 25.9 us -> 23.6 us (0.911)
  local copies, waits for them, and re-layouts: 4 us -> 1.26 us
  Pallas kernels: 21.5 us -> 22.1 us
    unnamed x11 -> x1, local copies, waits for them, and re-layouts: 4 us -> 1.26 us
    pallas_call x1, Pallas kernels: 21.5 us -> 22.1 us  [per_device(): pl.pallas_call(functools.partial(fused_kernel, n), out_shape=jax.ShapeDty...]
where the time goes in v2:
time: 23.6 us; the launch traced here: 23.4 us
  Pallas kernels  22.1 us (94%)
  local copies, waits for them, and re-layouts  1.26 us (5%)
    pallas_call x1, Pallas kernels, per_device(): pl.pallas_call(functools.partial(fused_kernel, n), out_shape=jax.ShapeDty...  22.1 us
    unnamed x1, local copies, waits for them, and re-layouts  1.26 us

profile of v2, /device:TPU:0, one launch (start us, length us, event | category | flops | bytes accessed | tf_op | source)
XLA Modules:
  0.0 23.4 jit_solution(14950649172113042394)
XLA Ops:
  0.0 22.1 %paged_sparse_decode.1 = bf16[4,256]{1,0:T(4,128)(2,1)} custom-call(bf16[4,256]{1,0:T(4,128)(2,1)} %q_hbm.1, f32[4,64]{1,0:T(4,128)} %gate_hbm.1, bf16[16,128,2048]{2,1,0:T(8,128)(2,1)} %kv_hbm.1, s32[4,64]{1,0:T(4,128)} %pt_hbm.1, s32[4,8,16]{2,1,0:T(8,128)} %sel_hbm.1, s32[4]{0:T(128)} %len_hbm.1), custom_call_target="tpu_custom_call" | custom-call | tf_op jit(solution)/shard_map/paged_sparse_decode/pallas_call | solution.py:381
  22.1 1.3 %copy.8 = bf16[4,256]{1,0:T(4,128)(2,1)} copy(bf16[4,256]{1,0:T(4,128)(2,1)} %paged_sparse_decode.1) | data formatting | bytes 4096

commit v3 on v2

--- a/solution.py
+++ b/solution.py
@@ -137,7 +137,7 @@
 
 def fused_kernel(
     n, q_hbm, gate_hbm, kv_hbm, pt_hbm, sel_hbm, len_hbm, out_ref,
-    kv_buf, q_all, gate_v, pt_v, sel_v, len_s, q_even, gather_f, send_buf, recv_buf,
+    kv_buf, q_all, gate_v, pt_v, sel_v, len_s, q_even, sum_k, sum_v, gather_f, send_buf, recv_buf,
     kv_sem, in_sem, q_send, q_recv, p_send, p_recv,
 ):
     me = lax.axis_index("seq")
@@ -229,6 +229,26 @@
         live.append(live_j)
         count.append(count_j)
 
+    row16 = lax.broadcasted_iota(jnp.int32, (16, span), 0)
+
+    def by_head(row):
+        wide = jnp.broadcast_to(row[:, :HEAD_DIM], (heads, HEAD_DIM))
+        for k in range(1, kv_heads):
+            wide = jnp.where(kv_row == k, row[:, k * HEAD_DIM : (k + 1) * HEAD_DIM], wide)
+        return wide
+
+    for j in range(runs):
+        load_run(j).wait()
+        page_rows = jnp.where(lane // page_len == row16, valid[j], 0.0).astype(BF16)
+        sums = jnp.dot(
+            page_rows, kv_buf[j * RUN : (j + 1) * RUN].reshape(span, width),
+            preferred_element_type=F32,
+        )
+        for e in range(RUN):
+            mean = (sums[e : e + 1, :] / count[j][e]).astype(BF16).astype(F32)
+            sum_k[j * RUN + e] = by_head(mean[:, :kv_width])
+            sum_v[j * RUN + e] = by_head(mean[:, kv_width:])
+
     for step, peer in enumerate(peers):
         q_copy(peer, peer).wait_recv()
     for src in range(n):
@@ -243,86 +263,107 @@
         )
         for r in range(requests)
     ]
-
-    fine_m, fine_l, fine_n, coarse_s, coarse_v = [], [], [], [], []
-    valid_rows = 16
-    row16 = lax.broadcasted_iota(jnp.int32, (valid_rows, span), 0)
+    kv_col = jnp.broadcast_to(kv_row, (heads, HEAD_DIM))
+    own = [jnp.where(kv_col == k, 1.0, 0.0).astype(BF16) for k in range(kv_heads)]
+
+    scores, coarse_s = [], []
     for j in range(runs):
         q_j = q_rows[0] * hot[j][0]
         for r in range(1, requests):
             q_j = q_j + q_rows[r] * hot[j][r]
-        q_bd = jnp.concatenate(
-            [jnp.where(kv_row == k, q_j, 0.0) for k in range(kv_heads)], axis=1
-        ).astype(BF16)
-        load_run(j).wait()
+        q_b = q_j.astype(BF16)
+        q_bd = jnp.concatenate([q_b * own[k] for k in range(kv_heads)], axis=1)
         keys = kv_buf[j * RUN : (j + 1) * RUN, :, :kv_width].reshape(span, kv_width)
-        vals = kv_buf[j * RUN : (j + 1) * RUN, :, kv_width:].reshape(span, kv_width)
-        scores = lax.dot_general(
-            q_bd, keys, (((1,), (1,)), ((), ())), preferred_element_type=F32
-        ) * scale
+        scores.append(
+            lax.dot_general(
+                q_bd, keys, (((1,), (1,)), ((), ())), preferred_element_type=F32
+            )
+        )
+        pair = []
+        for e in range(RUN):
+            dot = jnp.sum(q_j * sum_k[j * RUN + e], axis=1, keepdims=True) * scale
+            pair.append(jnp.where(live[j][e] > 0.0, dot, neg_big))
+        coarse_s.append(pair)
+    fine_m, fine_l, weights = [], [], []
+    for j in range(runs):
         ok = fine_ok[j] > 0.0
-        masked = jnp.where(ok, scores, neg_big)
+        masked = jnp.where(ok, scores[j] * scale, neg_big)
         top = jnp.max(masked, axis=1, keepdims=True)
         wt = jnp.where(ok, jnp.exp2(masked - top), 0.0).astype(BF16)
         fine_m.append(top)
         fine_l.append(jnp.sum(wt.astype(F32), axis=1, keepdims=True))
-        shown = scores * valid[j]
-        page_rows = jnp.where(lane // page_len == row16, valid[j], 0.0).astype(BF16)
-        mixed = lax.dot_general(
-            jnp.concatenate([wt, page_rows], axis=0), vals, (((1,), (0,)), ((), ())),
-            preferred_element_type=F32,
-        )
-        num = mixed[:heads, :HEAD_DIM]
+        weights.append(wt)
+    fine_n = []
+    for j in range(runs):
+        vals = kv_buf[j * RUN : (j + 1) * RUN, :, kv_width:].reshape(span, kv_width)
+        mixed = jnp.dot(weights[j], vals, preferred_element_type=F32)
+        num = mixed[:, :HEAD_DIM]
         for k in range(1, kv_heads):
-            num = jnp.where(kv_row == k, mixed[:heads, k * HEAD_DIM : (k + 1) * HEAD_DIM], num)
+            num = jnp.where(kv_row == k, mixed[:, k * HEAD_DIM : (k + 1) * HEAD_DIM], num)
         fine_n.append(num)
-        for e in range(RUN):
-            mean = jnp.sum(
-                shown[:, e * page_len : (e + 1) * page_len], axis=1, keepdims=True
-            ) / count[j][e]
-            coarse_s.append(jnp.where(live[j][e] > 0.0, mean, neg_big))
-            sv = (mixed[heads + e : heads + e + 1, :] / count[j][e]).astype(BF16).astype(F32)
-            wide = jnp.broadcast_to(sv[:, :HEAD_DIM], (heads, HEAD_DIM))
-            for k in range(1, kv_heads):
-                wide = jnp.where(kv_row == k, sv[:, k * HEAD_DIM : (k + 1) * HEAD_DIM], wide)
-            coarse_v.append(wide)
-
-    unit = 2 * per_dev * requests
-    lane_row = lax.broadcasted_iota(jnp.int32, (heads, HEAD_DIM), 1)
-
-    def put(kind, r, top, total, num):
-        top_b = top.astype(BF16).astype(F32)
-        high = total.astype(BF16).astype(F32)
-        stat = jnp.where(lane_row == 0, top_b, jnp.where(lane_row == 1, high, total - high))
+
+    kind_rows = per_dev * requests
+    unit = 2 * kind_rows
+    rows_out = unit + kind_rows
+    lane_id = lax.broadcasted_iota(jnp.int32, (heads, HEAD_DIM), 1)
+
+    def request_tops(run_tops):
+        tops = []
+        for r in range(requests):
+            held = [jnp.where(hot[j][r] > 0.0, run_tops[j], neg_big) for j in range(runs)]
+            tops.append(functools.reduce(jnp.maximum, held).astype(BF16).astype(F32))
+        return tops
+
+    def of_run(tops, j):
+        mine = tops[0] * hot[j][0]
+        for r in range(1, requests):
+            mine = mine + tops[r] * hot[j][r]
+        return mine
+
+    def weight_of(score, base):
+        return jnp.where(score > 0.5 * neg_big, jnp.exp2(score - base), 0.0)
+
+    def split_by_request(parts):
+        totals = []
+        for r in range(requests):
+            total = parts[0] * hot[0][r]
+            for j in range(1, runs):
+                total = total + parts[j] * hot[j][r]
+            totals.append(total)
+        return totals
+
+    coarse_tops = request_tops([functools.reduce(jnp.maximum, pair) for pair in coarse_s])
+    coarse_sum, coarse_num = [], []
+    for j in range(runs):
+        base = of_run(coarse_tops, j)
+        wts = [weight_of(s, base) for s in coarse_s[j]]
+        coarse_sum.append(functools.reduce(jnp.add, wts))
+        coarse_num.append(
+            functools.reduce(jnp.add, [wts[e] * sum_v[j * RUN + e] for e in range(RUN)])
+        )
+    fine_tops = request_tops(fine_m)
+    fine_sum, fine_num = [], []
+    for j in range(runs):
+        wt = weight_of(fine_m[j], of_run(fine_tops, j))
+        fine_sum.append(wt * fine_l[j])
+        fine_num.append(wt * fine_n[j])
+    tops = [coarse_tops, fine_tops]
+    sums = [split_by_request(coarse_sum), split_by_request(fine_sum)]
+    nums = [split_by_request(coarse_num), split_by_request(fine_num)]
+    for r in range(requests):
+        stat = jnp.zeros((heads, HEAD_DIM), F32)
+        for kind in range(2):
+            high = sums[kind][r].astype(BF16).astype(F32)
+            for i, value in enumerate((tops[kind][r], high, sums[kind][r] - high)):
+                stat = jnp.where(lane_id == 3 * kind + i, value, stat)
         for w in range(per_dev):
-            row = kind * per_dev * requests + w * requests + r
-            gather_f[pl.ds(row, n, stride=2 * unit), :] = num[w * n : (w + 1) * n]
-            gather_f[pl.ds(unit + row, n, stride=2 * unit), :] = stat[w * n : (w + 1) * n]
-
-    for r in range(requests):
-        for kind in range(2):
-            if kind == 0:
-                tops = coarse_s
-                owner = [hot[i // RUN][r] for i in range(slots)]
-            else:
-                tops = fine_m
-                owner = [hot[j][r] for j in range(runs)]
-            held = [jnp.where(o > 0.0, t, neg_big) for o, t in zip(owner, tops)]
-            top = functools.reduce(jnp.maximum, held)
-            top = top.astype(BF16).astype(F32)
-            total = jnp.zeros((heads, 1), F32)
-            num = jnp.zeros((heads, HEAD_DIM), F32)
-            for i, h in enumerate(held):
-                weight = jnp.where(h > 0.5 * neg_big, jnp.exp2(h - top), 0.0)
-                if kind == 0:
-                    total = total + weight
-                    num = num + weight * coarse_v[i]
-                else:
-                    total = total + weight * fine_l[i]
-                    num = num + weight * fine_n[i]
-            put(kind, r, top, total, num)
+            part = slice(w * n, (w + 1) * n)
+            row = w * requests + r
+            for kind in range(2):
+                gather_f[pl.ds(kind * kind_rows + row, n, stride=rows_out), :] = nums[kind][r][part]
+            gather_f[pl.ds(unit + row, n, stride=rows_out), :] = stat[part]
     for d in range(n):
-        send_buf[d] = gather_f[d * 2 * unit : (d + 1) * 2 * unit, :].astype(BF16)
+        send_buf[d] = gather_f[d * rows_out : (d + 1) * rows_out, :].astype(BF16)
 
     def p_copy(slot, peer):
         return pltpu.make_async_remote_copy(
@@ -348,21 +389,23 @@
     for peer in peers:
         p_copy(peer, peer).wait_recv()
     stats = [recv_buf[src, unit:, :].astype(F32) for src in range(n)]
-    tops = [s[:, 0:1] for s in stats]
-    top = functools.reduce(jnp.maximum, tops)
-    total = jnp.zeros((unit, 1), F32)
-    num = jnp.zeros((unit, HEAD_DIM), F32)
-    for src in range(n):
-        weight = jnp.exp2(tops[src] - top)
-        total = total + weight * (stats[src][:, 1:2] + stats[src][:, 2:3])
-        num = num + weight * recv_buf[src, :unit, :].astype(F32)
-    full = num / total
+    full = []
+    for kind in range(2):
+        tops = [s[:, 3 * kind : 3 * kind + 1] for s in stats]
+        top = functools.reduce(jnp.maximum, tops)
+        total = jnp.zeros((kind_rows, 1), F32)
+        num = jnp.zeros((kind_rows, HEAD_DIM), F32)
+        part = slice(kind * kind_rows, (kind + 1) * kind_rows)
+        for src in range(n):
+            weight = jnp.exp2(tops[src] - top)
+            both = stats[src][:, 3 * kind + 1 : 3 * kind + 2] + stats[src][:, 3 * kind + 2 : 3 * kind + 3]
+            total = total + weight * both
+            num = num + weight * recv_buf[src, part, :].astype(F32)
+        full.append(num / total)
     for w in range(per_dev):
-        c_row = w * requests
-        f_row = per_dev * requests + w * requests
+        part = slice(w * requests, (w + 1) * requests)
         out_ref[:, w * HEAD_DIM : (w + 1) * HEAD_DIM] = (
-            gate_col[0][w] * full[c_row : c_row + requests]
-            + gate_col[1][w] * full[f_row : f_row + requests]
+            gate_col[0][w] * full[0][part] + gate_col[1][w] * full[1][part]
         ).astype(BF16)
     for peer in peers:
         q_copy(me, peer).wait_send()
@@ -376,7 +419,7 @@
     if cols % HEAD_DIM != 0:
         return per_device_plain(queries, gate_logits, kv_pool, page_table, selected, lengths)
     per_dev = cols // HEAD_DIM
-    unit = 2 * per_dev * requests
+    rows_out = 3 * per_dev * requests
     dma = pltpu.SemaphoreType.DMA
     return pl.pallas_call(
         functools.partial(fused_kernel, n),
@@ -391,9 +434,11 @@
             pltpu.VMEM(selected.shape, jnp.int32),
             pltpu.SMEM(lengths.shape, jnp.int32),
             pltpu.VMEM((per_dev, n * requests, HEAD_DIM), F32),
-            pltpu.VMEM((n * 2 * unit, HEAD_DIM), F32),
-            pltpu.VMEM((n, 2 * unit, HEAD_DIM), BF16),
-            pltpu.VMEM((n, 2 * unit, HEAD_DIM), BF16),
+            pltpu.VMEM((slots, per_dev * n, HEAD_DIM), F32),
+            pltpu.VMEM((slots, per_dev * n, HEAD_DIM), F32),
+            pltpu.VMEM((n * rows_out, HEAD_DIM), F32),
+            pltpu.VMEM((n, rows_out, HEAD_DIM), BF16),
+            pltpu.VMEM((n, rows_out, HEAD_DIM), BF16),
             dma((slots // RUN,)),
             dma((5,)),
             dma((n,)),

time: 23.6 us -> 19.6 us (0.83)
  Pallas kernels: 22.1 us -> 18.2 us
    pallas_call x1, Pallas kernels: 22.1 us -> 18.2 us  [per_device(): pl.pallas_call(functools.partial(fused_kernel, n), out_shape=jax.ShapeDty...]
where the time goes in v3:
time: 19.6 us; the launch traced here: 19.5 us
  Pallas kernels  18.2 us (93%)
  local copies, waits for them, and re-layouts  1.26 us (6%)
    pallas_call x1, Pallas kernels, per_device(): pl.pallas_call(functools.partial(fused_kernel, n), out_shape=jax.ShapeDty...  18.2 us
    unnamed x1, local copies, waits for them, and re-layouts  1.26 us

profile of v3, /device:TPU:0, one launch (start us, length us, event | category | flops | bytes accessed | tf_op | source)
XLA Modules:
  0.0 19.5 jit_solution(5467412861577978667)
XLA Ops:
  0.0 18.2 %paged_sparse_decode.1 = bf16[4,256]{1,0:T(4,128)(2,1)} custom-call(bf16[4,256]{1,0:T(4,128)(2,1)} %q_hbm.1, f32[4,64]{1,0:T(4,128)} %gate_hbm.1, bf16[16,128,2048]{2,1,0:T(8,128)(2,1)} %kv_hbm.1, s32[4,64]{1,0:T(4,128)} %pt_hbm.1, s32[4,8,16]{2,1,0:T(8,128)} %sel_hbm.1, s32[4]{0:T(128)} %len_hbm.1), custom_call_target="tpu_custom_call" | custom-call | tf_op jit(solution)/shard_map/paged_sparse_decode/pallas_call | solution.py:424
  18.2 1.3 %copy.8 = bf16[4,256]{1,0:T(4,128)(2,1)} copy(bf16[4,256]{1,0:T(4,128)(2,1)} %paged_sparse_decode.1) | data formatting | bytes 4096

commit v4 on v3

--- a/solution.py
+++ b/solution.py
@@ -284,6 +284,70 @@
             dot = jnp.sum(q_j * sum_k[j * RUN + e], axis=1, keepdims=True) * scale
             pair.append(jnp.where(live[j][e] > 0.0, dot, neg_big))
         coarse_s.append(pair)
+    kind_rows = per_dev * requests
+    rows_out = kind_rows + 1
+    lane_id = lax.broadcasted_iota(jnp.int32, (n, HEAD_DIM), 1)
+
+    def request_tops(run_tops):
+        tops = []
+        for r in range(requests):
+            held = [jnp.where(hot[j][r] > 0.0, run_tops[j], neg_big) for j in range(runs)]
+            tops.append(functools.reduce(jnp.maximum, held).astype(BF16).astype(F32))
+        return tops
+
+    def of_run(tops, j):
+        mine = tops[0] * hot[j][0]
+        for r in range(1, requests):
+            mine = mine + tops[r] * hot[j][r]
+        return mine
+
+    def weight_of(score, base):
+        return jnp.where(score > 0.5 * neg_big, jnp.exp2(score - base), 0.0)
+
+    def split_by_request(parts):
+        totals = []
+        for r in range(requests):
+            total = parts[0] * hot[0][r]
+            for j in range(1, runs):
+                total = total + parts[j] * hot[j][r]
+            totals.append(total)
+        return totals
+
+    coarse_tops = request_tops([functools.reduce(jnp.maximum, pair) for pair in coarse_s])
+    coarse_sum, coarse_num = [], []
+    for j in range(runs):
+        base = of_run(coarse_tops, j)
+        wts = [weight_of(s, base) for s in coarse_s[j]]
+        coarse_sum.append(functools.reduce(jnp.add, wts))
+        coarse_num.append(
+            functools.reduce(jnp.add, [wts[e] * sum_v[j * RUN + e] for e in range(RUN)])
+        )
+    def p_copy(kind, slot, peer):
+        return pltpu.make_async_remote_copy(
+            src_ref=send_buf.at[kind, peer], dst_ref=recv_buf.at[kind, slot],
+            send_sem=p_send.at[kind, peer], recv_sem=p_recv.at[kind, slot],
+            device_id={"seq": peer}, device_id_type=MESH,
+        )
+
+    def send_partials(kind, tops, sums, nums):
+        stat = jnp.zeros((n, HEAD_DIM), F32)
+        for r in range(requests):
+            high = sums[r].astype(BF16).astype(F32)
+            for w in range(per_dev):
+                part = slice(w * n, (w + 1) * n)
+                row = w * requests + r
+                gather_f[pl.ds(row, n, stride=rows_out), :] = nums[r][part]
+                for i, value in enumerate((tops[r], high, sums[r] - high)):
+                    stat = jnp.where(lane_id == i * kind_rows + row, value[part], stat)
+        gather_f[pl.ds(kind_rows, n, stride=rows_out), :] = stat
+        for d in range(n):
+            send_buf[kind, d] = gather_f[d * rows_out : (d + 1) * rows_out, :].astype(BF16)
+        for peer in peers:
+            p_copy(kind, me, peer).start()
+        recv_buf[kind, me] = send_buf[kind, me]
+
+    send_partials(0, coarse_tops, split_by_request(coarse_sum), split_by_request(coarse_num))
+
     fine_m, fine_l, weights = [], [], []
     for j in range(runs):
         ok = fine_ok[j] > 0.0
@@ -302,78 +366,14 @@
             num = jnp.where(kv_row == k, mixed[:, k * HEAD_DIM : (k + 1) * HEAD_DIM], num)
         fine_n.append(num)
 
-    kind_rows = per_dev * requests
-    unit = 2 * kind_rows
-    rows_out = unit + kind_rows
-    lane_id = lax.broadcasted_iota(jnp.int32, (heads, HEAD_DIM), 1)
-
-    def request_tops(run_tops):
-        tops = []
-        for r in range(requests):
-            held = [jnp.where(hot[j][r] > 0.0, run_tops[j], neg_big) for j in range(runs)]
-            tops.append(functools.reduce(jnp.maximum, held).astype(BF16).astype(F32))
-        return tops
-
-    def of_run(tops, j):
-        mine = tops[0] * hot[j][0]
-        for r in range(1, requests):
-            mine = mine + tops[r] * hot[j][r]
-        return mine
-
-    def weight_of(score, base):
-        return jnp.where(score > 0.5 * neg_big, jnp.exp2(score - base), 0.0)
-
-    def split_by_request(parts):
-        totals = []
-        for r in range(requests):
-            total = parts[0] * hot[0][r]
-            for j in range(1, runs):
-                total = total + parts[j] * hot[j][r]
-            totals.append(total)
-        return totals
-
-    coarse_tops = request_tops([functools.reduce(jnp.maximum, pair) for pair in coarse_s])
-    coarse_sum, coarse_num = [], []
-    for j in range(runs):
-        base = of_run(coarse_tops, j)
-        wts = [weight_of(s, base) for s in coarse_s[j]]
-        coarse_sum.append(functools.reduce(jnp.add, wts))
-        coarse_num.append(
-            functools.reduce(jnp.add, [wts[e] * sum_v[j * RUN + e] for e in range(RUN)])
-        )
     fine_tops = request_tops(fine_m)
     fine_sum, fine_num = [], []
     for j in range(runs):
         wt = weight_of(fine_m[j], of_run(fine_tops, j))
         fine_sum.append(wt * fine_l[j])
         fine_num.append(wt * fine_n[j])
-    tops = [coarse_tops, fine_tops]
-    sums = [split_by_request(coarse_sum), split_by_request(fine_sum)]
-    nums = [split_by_request(coarse_num), split_by_request(fine_num)]
-    for r in range(requests):
-        stat = jnp.zeros((heads, HEAD_DIM), F32)
-        for kind in range(2):
-            high = sums[kind][r].astype(BF16).astype(F32)
-            for i, value in enumerate((tops[kind][r], high, sums[kind][r] - high)):
-                stat = jnp.where(lane_id == 3 * kind + i, value, stat)
-        for w in range(per_dev):
-            part = slice(w * n, (w + 1) * n)
-            row = w * requests + r
-            for kind in range(2):
-                gather_f[pl.ds(kind * kind_rows + row, n, stride=rows_out), :] = nums[kind][r][part]
-            gather_f[pl.ds(unit + row, n, stride=rows_out), :] = stat[part]
-    for d in range(n):
-        send_buf[d] = gather_f[d * rows_out : (d + 1) * rows_out, :].astype(BF16)
-
-    def p_copy(slot, peer):
-        return pltpu.make_async_remote_copy(
-            src_ref=send_buf.at[peer], dst_ref=recv_buf.at[slot], send_sem=p_send.at[peer],
-            recv_sem=p_recv.at[slot], device_id={"seq": peer}, device_id_type=MESH,
-        )
-
-    for peer in peers:
-        p_copy(me, peer).start()
-    recv_buf[me] = send_buf[me]
+    send_partials(1, fine_tops, split_by_request(fine_sum), split_by_request(fine_num))
+
     gates = jax.nn.sigmoid(gate_v[...])
     gate_lane = lax.broadcasted_iota(jnp.int32, gates.shape, 1)
     gate_col = [
@@ -386,22 +386,22 @@
         ]
         for kind in range(2)
     ]
-    for peer in peers:
-        p_copy(peer, peer).wait_recv()
-    stats = [recv_buf[src, unit:, :].astype(F32) for src in range(n)]
     full = []
     for kind in range(2):
-        tops = [s[:, 3 * kind : 3 * kind + 1] for s in stats]
-        top = functools.reduce(jnp.maximum, tops)
-        total = jnp.zeros((kind_rows, 1), F32)
+        for peer in peers:
+            p_copy(kind, peer, peer).wait_recv()
+        stats = jnp.concatenate(
+            [recv_buf[kind, src, kind_rows:, :].astype(F32) for src in range(n)], axis=0
+        )
+        tops = stats[:, :kind_rows]
+        weight = jnp.exp2(tops - jnp.max(tops, axis=0, keepdims=True))
+        both = stats[:, kind_rows : 2 * kind_rows] + stats[:, 2 * kind_rows : 3 * kind_rows]
+        weight = weight / jnp.sum(weight * both, axis=0, keepdims=True)
+        weight = weight.T
         num = jnp.zeros((kind_rows, HEAD_DIM), F32)
-        part = slice(kind * kind_rows, (kind + 1) * kind_rows)
         for src in range(n):
-            weight = jnp.exp2(tops[src] - top)
-            both = stats[src][:, 3 * kind + 1 : 3 * kind + 2] + stats[src][:, 3 * kind + 2 : 3 * kind + 3]
-            total = total + weight * both
-            num = num + weight * recv_buf[src, part, :].astype(F32)
-        full.append(num / total)
+            num = num + weight[:, src : src + 1] * recv_buf[kind, src, :kind_rows, :].astype(F32)
+        full.append(num)
     for w in range(per_dev):
         part = slice(w * requests, (w + 1) * requests)
         out_ref[:, w * HEAD_DIM : (w + 1) * HEAD_DIM] = (
@@ -409,7 +409,8 @@
         ).astype(BF16)
     for peer in peers:
         q_copy(me, peer).wait_send()
-        p_copy(me, peer).wait_send()
+        p_copy(0, me, peer).wait_send()
+        p_copy(1, me, peer).wait_send()
 
 
 def per_device(queries, gate_logits, kv_pool, page_table, selected, lengths):
@@ -419,7 +420,7 @@
     if cols % HEAD_DIM != 0:
         return per_device_plain(queries, gate_logits, kv_pool, page_table, selected, lengths)
     per_dev = cols // HEAD_DIM
-    rows_out = 3 * per_dev * requests
+    rows_out = per_dev * requests + 1
     dma = pltpu.SemaphoreType.DMA
     return pl.pallas_call(
         functools.partial(fused_kernel, n),
@@ -437,14 +438,14 @@
             pltpu.VMEM((slots, per_dev * n, HEAD_DIM), F32),
             pltpu.VMEM((slots, per_dev * n, HEAD_DIM), F32),
             pltpu.VMEM((n * rows_out, HEAD_DIM), F32),
-            pltpu.VMEM((n, rows_out, HEAD_DIM), BF16),
-            pltpu.VMEM((n, rows_out, HEAD_DIM), BF16),
+            pltpu.VMEM((2, n, rows_out, HEAD_DIM), BF16),
+            pltpu.VMEM((2, n, rows_out, HEAD_DIM), BF16),
             dma((slots // RUN,)),
             dma((5,)),
             dma((n,)),
             dma((n,)),
-            dma((n,)),
-            dma((n,)),
+            dma((2, n)),
+            dma((2, n)),
         ],
         compiler_params=pltpu.CompilerParams(
             collective_id=0, has_side_effects=True, vmem_limit_bytes=67043328

time: 19.6 us -> 19.9 us (1.015)
  Pallas kernels: 18.2 us -> 18.4 us
    pallas_call x1, Pallas kernels: 18.2 us -> 18.4 us  [per_device(): pl.pallas_call(functools.partial(fused_kernel, n), out_shape=jax.ShapeDty...]
where the time goes in v4:
time: 19.9 us; the launch traced here: 19.7 us
  Pallas kernels  18.4 us (92%)
  local copies, waits for them, and re-layouts  1.26 us (6%)
    pallas_call x1, Pallas kernels, per_device(): pl.pallas_call(functools.partial(fused_kernel, n), out_shape=jax.ShapeDty...  18.4 us
    unnamed x1, local copies, waits for them, and re-layouts  1.26 us

profile of v4, /device:TPU:0, one launch (start us, length us, event | category | flops | bytes accessed | tf_op | source)
XLA Modules:
  0.0 19.7 jit_solution(1457683573603604048)
XLA Ops:
  0.0 18.4 %paged_sparse_decode.1 = bf16[4,256]{1,0:T(4,128)(2,1)} custom-call(bf16[4,256]{1,0:T(4,128)(2,1)} %q_hbm.1, f32[4,64]{1,0:T(4,128)} %gate_hbm.1, bf16[16,128,2048]{2,1,0:T(8,128)(2,1)} %kv_hbm.1, s32[4,64]{1,0:T(4,128)} %pt_hbm.1, s32[4,8,16]{2,1,0:T(8,128)} %sel_hbm.1, s32[4]{0:T(128)} %len_hbm.1), custom_call_target="tpu_custom_call" | custom-call | tf_op jit(solution)/shard_map/paged_sparse_decode/pallas_call | solution.py:425
  18.4 1.3 %copy.8 = bf16[4,256]{1,0:T(4,128)(2,1)} copy(bf16[4,256]{1,0:T(4,128)(2,1)} %paged_sparse_decode.1) | data formatting | bytes 4096

commit v5 on v3

--- a/solution.py
+++ b/solution.py
@@ -137,7 +137,7 @@
 
 def fused_kernel(
     n, q_hbm, gate_hbm, kv_hbm, pt_hbm, sel_hbm, len_hbm, out_ref,
-    kv_buf, q_all, gate_v, pt_v, sel_v, len_s, q_even, sum_k, sum_v, gather_f, send_buf, recv_buf,
+    kv_buf, q_all, gate_v, pt_v, sel_v, len_s, q_even, score_v, sum_k, sum_v, gather_f, send_buf, recv_buf,
     kv_sem, in_sem, q_send, q_recv, p_send, p_recv,
 ):
     me = lax.axis_index("seq")
@@ -165,7 +165,9 @@
         pltpu.make_async_copy(gate_hbm, gate_v, in_sem.at[4]),
     ]
     barrier = pltpu.get_barrier_semaphore()
-    peers = [lax.rem(me + step, n) for step in range(1, n)]
+    peers = [
+        lax.rem(me + step, n) for step in sorted(range(1, n), key=lambda s: min(s, n - s))
+    ]
     for peer in peers:
         pl.semaphore_signal(barrier, inc=1, device_id={"seq": peer}, device_id_type=MESH)
     for copy in small:
@@ -249,36 +251,68 @@
             sum_k[j * RUN + e] = by_head(mean[:, :kv_width])
             sum_v[j * RUN + e] = by_head(mean[:, kv_width:])
 
-    for step, peer in enumerate(peers):
-        q_copy(peer, peer).wait_recv()
-    for src in range(n):
-        rows = q_all[src].astype(F32)
+    half = n // 2
+    half_heads = kv_heads // 2
+    half_width = half_heads * HEAD_DIM
+    my_half = me // half
+    half_row = lax.broadcasted_iota(jnp.int32, (per_dev * half, HEAD_DIM), 0)
+    half_kv = (lax.rem(half_row, half) * per_dev + half_row // half) // group
+    own = [jnp.where(half_kv == k, 1.0, 0.0).astype(BF16) for k in range(half_heads)]
+    parts = []
+    for stage in range(2):
+        which = my_half if stage == 0 else 1 - my_half
+        if stage == 0:
+            for step in range(1, half):
+                near = my_half * half + lax.rem(lax.rem(me, half) + step, half)
+                q_copy(near, near).wait_recv()
+        else:
+            for i in range(half):
+                q_copy(which * half + i, which * half + i).wait_recv()
+        for i in range(half):
+            rows = q_all[which * half + i].astype(F32)
+            for w in range(per_dev):
+                q_even[stage, w, i * requests : (i + 1) * requests, :] = rows[
+                    :, w * HEAD_DIM : (w + 1) * HEAD_DIM
+                ]
+        part = [
+            jnp.concatenate(
+                [q_even[stage, w, pl.ds(r, half, stride=requests), :] for w in range(per_dev)],
+                axis=0,
+            )
+            for r in range(requests)
+        ]
+        parts.append(part)
+        first_col = pl.multiple_of(which * half_width, half_width)
+        for j in range(runs):
+            q_j = part[0] * hot[j][0]
+            for r in range(1, requests):
+                q_j = q_j + part[r] * hot[j][r]
+            q_b = q_j.astype(BF16)
+            q_bd = jnp.concatenate([q_b * own[k] for k in range(half_heads)], axis=1)
+            keys = kv_buf[j * RUN : (j + 1) * RUN, :, pl.ds(first_col, half_width)]
+            dots = lax.dot_general(
+                q_bd, keys.reshape(span, half_width), (((1,), (1,)), ((), ())),
+                preferred_element_type=F32,
+            )
+            for w in range(per_dev):
+                score_v[j, pl.ds(pl.multiple_of(w * n + which * half, 8), half), :] = dots[
+                    w * half : (w + 1) * half
+                ]
+    q_rows = []
+    for r in range(requests):
+        pieces = []
         for w in range(per_dev):
-            q_even[w, src * requests : (src + 1) * requests, :] = rows[
-                :, w * HEAD_DIM : (w + 1) * HEAD_DIM
-            ]
-    q_rows = [
-        jnp.concatenate(
-            [q_even[w, pl.ds(r, n, stride=requests), :] for w in range(per_dev)], axis=0
-        )
-        for r in range(requests)
-    ]
-    kv_col = jnp.broadcast_to(kv_row, (heads, HEAD_DIM))
-    own = [jnp.where(kv_col == k, 1.0, 0.0).astype(BF16) for k in range(kv_heads)]
+            near, far = [parts[stage][r][w * half : (w + 1) * half] for stage in range(2)]
+            pieces.append(jnp.where(my_half == 0, near, far))
+            pieces.append(jnp.where(my_half == 0, far, near))
+        q_rows.append(jnp.concatenate(pieces, axis=0))
 
     scores, coarse_s = [], []
     for j in range(runs):
         q_j = q_rows[0] * hot[j][0]
         for r in range(1, requests):
             q_j = q_j + q_rows[r] * hot[j][r]
-        q_b = q_j.astype(BF16)
-        q_bd = jnp.concatenate([q_b * own[k] for k in range(kv_heads)], axis=1)
-        keys = kv_buf[j * RUN : (j + 1) * RUN, :, :kv_width].reshape(span, kv_width)
-        scores.append(
-            lax.dot_general(
-                q_bd, keys, (((1,), (1,)), ((), ())), preferred_element_type=F32
-            )
-        )
+        scores.append(score_v[j])
         pair = []
         for e in range(RUN):
             dot = jnp.sum(q_j * sum_k[j * RUN + e], axis=1, keepdims=True) * scale
@@ -416,7 +450,7 @@
     n = lax.axis_size("seq")
     slots, page_len, width = kv_pool.shape
     requests, cols = queries.shape
-    if cols % HEAD_DIM != 0:
+    if cols % HEAD_DIM != 0 or n % 16 != 0:
         return per_device_plain(queries, gate_logits, kv_pool, page_table, selected, lengths)
     per_dev = cols // HEAD_DIM
     rows_out = 3 * per_dev * requests
@@ -433,7 +467,8 @@
             pltpu.VMEM(page_table.shape, jnp.int32),
             pltpu.VMEM(selected.shape, jnp.int32),
             pltpu.SMEM(lengths.shape, jnp.int32),
-            pltpu.VMEM((per_dev, n * requests, HEAD_DIM), F32),
+            pltpu.VMEM((2, per_dev, n // 2 * requests, HEAD_DIM), F32),
+            pltpu.VMEM((slots // RUN, per_dev * n, RUN * page_len), F32),
             pltpu.VMEM((slots, per_dev * n, HEAD_DIM), F32),
             pltpu.VMEM((slots, per_dev * n, HEAD_DIM), F32),
             pltpu.VMEM((n * rows_out, HEAD_DIM), F32),

time: 19.6 us -> 18.9 us (0.964)
  Pallas kernels: 18.2 us -> 17.5 us
    pallas_call x1, Pallas kernels: 18.2 us -> 17.5 us  [per_device(): pl.pallas_call(functools.partial(fused_kernel, n), out_shape=jax.ShapeDty...]
where the time goes in v5:
time: 18.9 us; the launch traced here: 18.7 us
  Pallas kernels  17.5 us (93%)
  local copies, waits for them, and re-layouts  1.26 us (7%)
    pallas_call x1, Pallas kernels, per_device(): pl.pallas_call(functools.partial(fused_kernel, n), out_shape=jax.ShapeDty...  17.5 us
    unnamed x1, local copies, waits for them, and re-layouts  1.26 us

profile of v5, /device:TPU:0, one launch (start us, length us, event | category | flops | bytes accessed | tf_op | source)
XLA Modules:
  0.0 18.7 jit_solution(12998533260044009409)
XLA Ops:
  0.0 17.5 %paged_sparse_decode.1 = bf16[4,256]{1,0:T(4,128)(2,1)} custom-call(bf16[4,256]{1,0:T(4,128)(2,1)} %q_hbm.1, f32[4,64]{1,0:T(4,128)} %gate_hbm.1, bf16[16,128,2048]{2,1,0:T(8,128)(2,1)} %kv_hbm.1, s32[4,64]{1,0:T(4,128)} %pt_hbm.1, s32[4,8,16]{2,1,0:T(8,128)} %sel_hbm.1, s32[4]{0:T(128)} %len_hbm.1), custom_call_target="tpu_custom_call" | custom-call | tf_op jit(solution)/shard_map/paged_sparse_decode/pallas_call | solution.py:458
  17.5 1.3 %copy.8 = bf16[4,256]{1,0:T(4,128)(2,1)} copy(bf16[4,256]{1,0:T(4,128)(2,1)} %paged_sparse_decode.1) | data formatting | bytes 4096

commit v6 on v5

--- a/solution.py
+++ b/solution.py
@@ -137,7 +137,7 @@
 
 def fused_kernel(
     n, q_hbm, gate_hbm, kv_hbm, pt_hbm, sel_hbm, len_hbm, out_ref,
-    kv_buf, q_all, gate_v, pt_v, sel_v, len_s, q_even, score_v, sum_k, sum_v, gather_f, send_buf, recv_buf,
+    kv_buf, q_all, gate_v, pt_v, sel_v, len_s, q_even, mask_v, sum_k, sum_v, gather_f, send_buf, recv_buf,
     kv_sem, in_sem, q_send, q_recv, p_send, p_recv,
 ):
     me = lax.axis_index("seq")
@@ -206,7 +206,7 @@
         chosen_ids.append(wide)
     lane = lax.broadcasted_iota(jnp.int32, (1, span), 1)
     lane_f = lane.astype(F32)
-    hot, valid, fine_ok, live, count = [], [], [], [], []
+    hot, valid, live, count = [], [], [], []
     for j in range(runs):
         match = table == me * slots + j * RUN
         page = jnp.sum(jnp.where(match, col_f, 0.0), axis=(0, 1), keepdims=True)
@@ -227,7 +227,7 @@
             count_j.append(jnp.clip(left, 1.0, float(page_len)))
         hot.append(hot_j)
         valid.append(valid_j)
-        fine_ok.append(ok * valid_j)
+        mask_v[j] = ok * valid_j
         live.append(live_j)
         count.append(count_j)
 
@@ -258,7 +258,7 @@
     half_row = lax.broadcasted_iota(jnp.int32, (per_dev * half, HEAD_DIM), 0)
     half_kv = (lax.rem(half_row, half) * per_dev + half_row // half) // group
     own = [jnp.where(half_kv == k, 1.0, 0.0).astype(BF16) for k in range(half_heads)]
-    parts = []
+    parts, fine_parts = [], []
     for stage in range(2):
         which = my_half if stage == 0 else 1 - my_half
         if stage == 0:
@@ -282,6 +282,7 @@
             for r in range(requests)
         ]
         parts.append(part)
+        dots_all = []
         first_col = pl.multiple_of(which * half_width, half_width)
         for j in range(runs):
             q_j = part[0] * hot[j][0]
@@ -294,48 +295,59 @@
                 q_bd, keys.reshape(span, half_width), (((1,), (1,)), ((), ())),
                 preferred_element_type=F32,
             )
-            for w in range(per_dev):
-                score_v[j, pl.ds(pl.multiple_of(w * n + which * half, 8), half), :] = dots[
-                    w * half : (w + 1) * half
-                ]
-    q_rows = []
-    for r in range(requests):
+            dots_all.append(dots)
+        wts = []
+        for j in range(runs):
+            dots = dots_all[j]
+            allowed = jnp.concatenate(
+                [
+                    mask_v[j, pl.ds(pl.multiple_of(w * n + which * half, 8), half), :]
+                    for w in range(per_dev)
+                ],
+                axis=0,
+            )
+            ok = allowed > 0.0
+            masked = jnp.where(ok, dots * scale, neg_big)
+            top = jnp.max(masked, axis=1, keepdims=True)
+            wt = jnp.where(ok, jnp.exp2(masked - top), 0.0).astype(BF16)
+            total = jnp.sum(wt.astype(F32), axis=1, keepdims=True)
+            wts.append((wt, top, total))
+        for j in range(runs):
+            wt, top, total = wts[j]
+            vals = kv_buf[
+                j * RUN : (j + 1) * RUN, :,
+                pl.ds(pl.multiple_of(kv_width + which * half_width, half_width), half_width),
+            ]
+            mixed = jnp.dot(wt, vals.reshape(span, half_width), preferred_element_type=F32)
+            num = mixed[:, :HEAD_DIM]
+            for k in range(1, half_heads):
+                num = jnp.where(half_kv == k, mixed[:, k * HEAD_DIM : (k + 1) * HEAD_DIM], num)
+            fine_parts.append((top, total, num))
+
+    def joined_halves(near, far):
         pieces = []
         for w in range(per_dev):
-            near, far = [parts[stage][r][w * half : (w + 1) * half] for stage in range(2)]
-            pieces.append(jnp.where(my_half == 0, near, far))
-            pieces.append(jnp.where(my_half == 0, far, near))
-        q_rows.append(jnp.concatenate(pieces, axis=0))
-
-    scores, coarse_s = [], []
+            part = slice(w * half, (w + 1) * half)
+            pieces.append(jnp.where(my_half == 0, near[part], far[part]))
+            pieces.append(jnp.where(my_half == 0, far[part], near[part]))
+        return jnp.concatenate(pieces, axis=0)
+
+    fine_m, fine_l, fine_n = [
+        [joined_halves(fine_parts[j][i], fine_parts[runs + j][i]) for j in range(runs)]
+        for i in range(3)
+    ]
+    q_rows = [joined_halves(parts[0][r], parts[1][r]) for r in range(requests)]
+
+    coarse_s = []
     for j in range(runs):
         q_j = q_rows[0] * hot[j][0]
         for r in range(1, requests):
             q_j = q_j + q_rows[r] * hot[j][r]
-        scores.append(score_v[j])
         pair = []
         for e in range(RUN):
             dot = jnp.sum(q_j * sum_k[j * RUN + e], axis=1, keepdims=True) * scale
             pair.append(jnp.where(live[j][e] > 0.0, dot, neg_big))
         coarse_s.append(pair)
-    fine_m, fine_l, weights = [], [], []
-    for j in range(runs):
-        ok = fine_ok[j] > 0.0
-        masked = jnp.where(ok, scores[j] * scale, neg_big)
-        top = jnp.max(masked, axis=1, keepdims=True)
-        wt = jnp.where(ok, jnp.exp2(masked - top), 0.0).astype(BF16)
-        fine_m.append(top)
-        fine_l.append(jnp.sum(wt.astype(F32), axis=1, keepdims=True))
-        weights.append(wt)
-    fine_n = []
-    for j in range(runs):
-        vals = kv_buf[j * RUN : (j + 1) * RUN, :, kv_width:].reshape(span, kv_width)
-        mixed = jnp.dot(weights[j], vals, preferred_element_type=F32)
-        num = mixed[:, :HEAD_DIM]
-        for k in range(1, kv_heads):
-            num = jnp.where(kv_row == k, mixed[:, k * HEAD_DIM : (k + 1) * HEAD_DIM], num)
-        fine_n.append(num)
-
     kind_rows = per_dev * requests
     unit = 2 * kind_rows
     rows_out = unit + kind_rows

time: 18.9 us -> 18.5 us (0.979)
  Pallas kernels: 17.5 us -> 17 us
    pallas_call x1, Pallas kernels: 17.5 us -> 17 us  [per_device(): pl.pallas_call(functools.partial(fused_kernel, n), out_shape=jax.ShapeDty...]
where the time goes in v6:
time: 18.5 us; the launch traced here: 18.3 us
  Pallas kernels  17 us (92%)
  local copies, waits for them, and re-layouts  1.26 us (7%)
    pallas_call x1, Pallas kernels, per_device(): pl.pallas_call(functools.partial(fused_kernel, n), out_shape=jax.ShapeDty...  17 us
    unnamed x1, local copies, waits for them, and re-layouts  1.26 us

profile of v6, /device:TPU:0, one launch (start us, length us, event | category | flops | bytes accessed | tf_op | source)
XLA Modules:
  0.0 18.3 jit_solution(17686210874348469247)
XLA Ops:
  0.0 17.0 %paged_sparse_decode.1 = bf16[4,256]{1,0:T(4,128)(2,1)} custom-call(bf16[4,256]{1,0:T(4,128)(2,1)} %q_hbm.1, f32[4,64]{1,0:T(4,128)} %gate_hbm.1, bf16[16,128,2048]{2,1,0:T(8,128)(2,1)} %kv_hbm.1, s32[4,64]{1,0:T(4,128)} %pt_hbm.1, s32[4,8,16]{2,1,0:T(8,128)} %sel_hbm.1, s32[4]{0:T(128)} %len_hbm.1), custom_call_target="tpu_custom_call" | custom-call | tf_op jit(solution)/shard_map/paged_sparse_decode/pallas_call | solution.py:470
  17.0 1.3 %copy.8 = bf16[4,256]{1,0:T(4,128)(2,1)} copy(bf16[4,256]{1,0:T(4,128)(2,1)} %paged_sparse_decode.1) | data formatting | bytes 4096
